TPU v7x, 256 devices: a 4x2x16 block of a 4x16x16 slice. The times are simulated.
256 devices in a mesh: pb: 2 (over y), col: 32 (over z, core), row: 4 (over x).
Axes of the slice: x: 4, y: 2, z: 16, core: 2. Of those that a mesh axis runs over, the one named last changes fastest.
The devices are a block of a 4x16x16 slice.
Arguments:
- pair_density: bfloat16 [6144, 6144], P(('pb', 'col'), 'row'), parts along dimension 0, may hold values from -0.19921875 to 0.19921875
- band_pairs: int32 [2, 3072], replicated, may hold values from 0 to 255, as said below
- valence: float32 [256], replicated, may hold values from -12 to -2
- conduction: float32 [12], replicated, may hold values from 1 to 8
- wave_vectors: int32 [3, 12288], P(None, 'pb'), parts along dimension 1, may hold values from -6 to 6
- momentum: float32 [6], P('pb'), parts along dimension 0, may hold values from 0.3 to 0.7
- guess_scale: float32 [12288], P('pb'), parts along dimension 0, may hold values from 0.4 to 0.75
Outputs:
- epsilon: float32 [12288, 6144], P(('pb', 'row'), 'col'), parts along dimension 0
- inverse: float32 [12288, 6144], P(('pb', 'row'), 'col'), parts along dimension 0
There are 2 independent parts, one for each index of `pb`. A program takes and returns all parts, laid end to end along the dimension named above; an argument that names none is the same for every part. Nothing has to cross between parts.
Inputs may be any that keep to these rules, and one draw needn't show every extreme that they name: `band_pairs`: column p names a valence band below 256 in row 0 and a conduction band below 12 in row 1; every such pair of bands appears in exactly one column.
All inputs are finite; a program needn't handle non-finite values.
Results may differ from a plain program's by a relative error of at most 0.0036.
The roundings to bfloat16 on the way count: a program that leaves them out, or rounds other values in their place, can miss the bound.
Values may be sent and summed in bfloat16 or wider, within the bound.
No kernel may reach another device: no remote copies, remote signals or barrier semaphores. Data moves between devices by JAX's collectives and lax.ppermute only.
A program may use at most 64 MiB of HBM per device.

v0:
```python
import math

import jax
import jax.numpy as jnp
from jax import lax
from jax.sharding import PartitionSpec as P


def copy_for_each(array, axis):
    copies = jnp.broadcast_to(array, (lax.axis_size(axis), *array.shape))
    return lax.all_to_all(copies, axis, split_axis=0, concat_axis=0, tiled=True)


def in_order(pieces, dim):
    lengths = list(pieces.shape[1:])
    lengths[dim] *= pieces.shape[0]
    return jnp.moveaxis(pieces, 0, dim).reshape(lengths)


def gathered_copies(array, axis, dim):
    pieces = copy_for_each(array, axis)
    return in_order(pieces, dim)


def lookup(indices, table):
    levels = jnp.arange(table.shape[0], dtype=jnp.int32)
    picked = indices[:, None] == levels[None, :]
    return jnp.sum(jnp.where(picked, table[None, :], 0.0), axis=1)


def on_device(pair_density, band_pairs, valence, conduction, wave_vectors, momentum, guess_scale):
    column_index = lax.axis_index("col")
    row_index = lax.axis_index("row")
    row_height = pair_density.shape[1]
    whole_width = row_height * lax.axis_size("row")
    strip_width = whole_width // lax.axis_size("col")
    valence_of = lookup(band_pairs[0], valence)
    conduction_of = lookup(band_pairs[1], conduction)
    weight = 4.0 / (valence_of - conduction_of)
    shifted = wave_vectors.astype(jnp.float32) + momentum[:, None]
    sqrt_all = jnp.sqrt(4.0 * math.pi / jnp.sum(shifted * shifted, axis=0))
    row_first = row_index * row_height
    column_first = column_index * strip_width
    sqrt_rows = lax.dynamic_slice_in_dim(sqrt_all, row_first, row_height, 0)
    sqrt_cols = lax.dynamic_slice_in_dim(sqrt_all, column_first, strip_width, 0)
    scale_rows = lax.dynamic_slice_in_dim(guess_scale, row_first, row_height, 0)
    scale_cols = lax.dynamic_slice_in_dim(guess_scale, column_first, strip_width, 0)
    panel_pairs = lax.all_gather(pair_density, "col", axis=0, tiled=True)
    owner = column_first // row_height
    offset = column_first % row_height
    own_slice = lax.dynamic_slice_in_dim(panel_pairs, offset, strip_width, 1)
    candidates = lax.all_gather(own_slice, "row", axis=1, tiled=True)
    strip_pairs = lax.dynamic_slice_in_dim(candidates, owner * strip_width, strip_width, 1)
    weighted = (weight[:, None] * panel_pairs.astype(jnp.float32)).astype(jnp.bfloat16)
    weighted_strip = (weight[:, None] * strip_pairs.astype(jnp.float32)).astype(jnp.bfloat16)
    chi_block = lax.dot_general(
        weighted, strip_pairs, (((0,), (0,)), ((), ())), preferred_element_type=jnp.float32
    )
    chi_rows = jnp.sum(weighted.astype(jnp.float32) * panel_pairs.astype(jnp.float32), axis=0)
    chi_cols = jnp.sum(weighted_strip.astype(jnp.float32) * strip_pairs.astype(jnp.float32), axis=0)
    global_rows = row_first + jnp.arange(row_height, dtype=jnp.int32)
    global_cols = column_first + jnp.arange(strip_width, dtype=jnp.int32)
    identity = (global_rows[:, None] == global_cols[None, :]).astype(jnp.float32)
    epsilon = identity - sqrt_rows[:, None] * chi_block * sqrt_cols[None, :]
    guess_rows = scale_rows / (1.0 - sqrt_rows * chi_rows * sqrt_rows)
    guess_cols = scale_cols / (1.0 - sqrt_cols * chi_cols * sqrt_cols)
    mixed = epsilon * guess_cols[None, :]
    mixed_b = mixed.astype(jnp.bfloat16)
    panel_mixed = lax.all_gather(mixed_b, "col", axis=1, tiled=True)
    strip_mixed = gathered_copies(mixed_b, "row", 0)
    square = jnp.dot(panel_mixed, strip_mixed, preferred_element_type=jnp.float32)
    square_b = square.astype(jnp.bfloat16)
    strip_square = gathered_copies(square_b, "row", 0)
    cube = jnp.dot(panel_mixed, strip_square, preferred_element_type=jnp.float32)
    inverse = guess_rows[:, None] * (4.0 * identity - 6.0 * mixed + 4.0 * square - cube)
    return (epsilon, inverse)


def solution(mesh):
    placed = (P(("pb", "col"), "row"), P(), P(), P(), P(None, "pb"), P("pb"), P("pb"))
    return jax.shard_map(
        on_device,
        mesh=mesh,
        in_specs=placed,
        out_specs=(P(("pb", "row"), "col"), P(("pb", "row"), "col")),
        check_vma=False,
    )
```

profile of v0, /device:TPU:33, one launch (start us, length us, event | category | flops | bytes accessed | tf_op | source)
XLA Modules:
  0.0 345.0 jit_solution(10228950458131673058)
XLA Ops:
  7.2 0.7 all-gather.4.cloned.1.call-update
  8.1 94.8 %all-gather.4.cloned.1.call-done = bf16[3072,1536]{1,0:T(8,128)(2,1)} async-done(((bf16[96,1536]{1,0:T(8,128)(2,1)}), bf16[3072,1536]{1,0:T(8,128)(2,1)}) %all-gather.4.cloned.1.call-update) | async-done | bytes 9437200 | tf_op jit(solution)/shard_map/all_gather | solution.py:48
  102.8 2.4 constant_dynamic-slice_fusion
  105.3 1.5 copy.18
  107.0 0.1 select_reduce_fusion.1
  107.2 0.1 multiply_reduce_fusion
  107.3 1.9 select_reduce_fusion
  109.2 6.2 %fusion.1 = f32[1536]{0:T(1024)S(1)} fusion(bf16[3072,1536]{1,0:T(8,128)(2,1)} %all-gather.4.cloned.1.call-done, f32[3072]{0:T(1024)S(1)} %subtract_divide_fusion), kind=kLoop, calls=%fused_computation.3 | loop fusion | flops 28310016 | bytes 9455616 | tf_op jit(solution)/shard_map/reduce_sum | solution.py:59
  115.5 0.8 fusion.20
  116.3 44.8 %all-gather.6.cloned.1.call-done = bf16[3072,768]{0,1:T(8,128)(2,1)} async-done(((bf16[3072,192]{0,1:T(8,128)(2,1)}), bf16[3072,768]{0,1:T(8,128)(2,1)}) %all-gather.6.cloned.1.call-update) | async-done | bytes 4718608 | tf_op jit(solution)/shard_map/all_gather | solution.py:52
  161.0 1.7 fusion.15
  162.7 0.8 fusion.22
  163.5 7.6 %multiply_convert_fusion = (bf16[1536,192]{0,1:T(8,128)(2,1)}, f32[1536,192]{0,1:T(8,128)}) fusion(f32[192]{0:T(256)S(1)} %get-tuple-element.4, f32[192]{0:T(256)S(1)} %get-tuple-element.5, bf16[3072,1536]{1,0:T(8,128)(2,1)} %all-gather.4.cloned.1.call-done, f32[3072]{0:T(1024)S(1)} %subtract_divide_fusion, ...), kind=kOutput, calls=%fused_computation.20 | convolution fusion | flops 1828159488 | bytes 12413188 | tf_op jit(solution)/shard_map/dot_general | solution.py:56
  171.2 1.2 broadcast_in_dim.47
  172.4 31.0 %all_to_all.10 = bf16[4,1536,192]{1,2,0:T(8,128)(2,1)S(1)} all-to-all(bf16[4,1536,192]{1,2,0:T(8,128)(2,1)S(1)} %broadcast_in_dim.47), channel_id=1, replica_groups=mesh['pb'=2,'col'=32,'row'=4] {'row'}, dimensions={0} | all-to-all | bytes 4718592 | tf_op jit(solution)/shard_map/all_to_all | solution.py:11
  203.5 0.3 copy.21
  203.7 84.0 %all-gather.8.cloned.1.call-done = bf16[1536,6144]{0,1:T(8,128)(2,1)} async-done(((bf16[1536,192]{0,1:T(8,128)(2,1)}), bf16[1536,6144]{0,1:T(8,128)(2,1)}) %all-gather.8.cloned.1.call-update) | async-done | bytes 18874384 | tf_op jit(solution)/shard_map/all_gather | solution.py:69
  287.8 11.4 %fusion.25 = (bf16[1536,192]{0,1:T(8,128)(2,1)S(1)}, f32[1536,192]{0,1:T(8,128)}) fusion(bf16[6144,192]{0,1:T(8,128)(2,1)S(1)} %bitcast.13, bf16[1536,6144]{0,1:T(8,128)(2,1)} %all-gather.8.cloned.1.call-done), kind=kOutput, calls=%fused_computation.38 | convolution fusion | flops 3624173568 | bytes 23003136 | tf_op jit(solution)/shard_map/dot_general | solution.py:71
  299.1 0.2 broadcast_in_dim.48
  299.3 32.6 %all_to_all.11 = bf16[4,1536,192]{1,2,0:T(8,128)(2,1)S(1)} all-to-all(bf16[4,1536,192]{1,2,0:T(8,128)(2,1)S(1)} %broadcast_in_dim.48), channel_id=1, replica_groups=mesh['pb'=2,'col'=32,'row'=4] {'row'}, dimensions={0} | all-to-all | bytes 4718592 | tf_op jit(solution)/shard_map/all_to_all | solution.py:11
  331.9 0.3 copy.22
  332.2 1.0 copy-done.5
  333.2 0.4 copy-done.6
  333.6 4.9 %fusion.13 = f32[1536,192]{0,1:T(8,128)} fusion(bf16[6144,192]{0,1:T(8,128)(2,1)S(1)} %bitcast.12, bf16[1536,6144]{0,1:T(8,128)(2,1)S(1)} %bitcast.17, f32[1536,192]{0,1:T(8,128)S(1)} %copy-done.6, f32[1536,192]{0,1:T(8,128)S(1)} %copy-done.5, f32[192]{0:T(256)S(1)} %get-tuple-element.4, f32[1536]{0:T(1024)S(1)} %get-tuple-element.2, ...), kind=kOutput, calls=%fused_computation.13 | convolution fusion | flops 3626532864 | bytes 24786432 | tf_op jit(solution)/shard_map/dot_general | solution.py:74
  (33 shorter events, 0.4 us)
Async XLA Ops:
  7.2 95.7 %all-gather.4.cloned.1.call-start = ((), (), s32[]{:S(2)}) async-start(), calls=%async_computation.2 | async-start | bytes 9732096 | tf_op jit(solution)/shard_map/all_gather | solution.py:48
  8.0 153.0 %all-gather.6.cloned.1.call-start = ((), (), s32[]{:S(2)}) async-start(), calls=%async_computation.3 | async-start | bytes 5898240 | tf_op jit(solution)/shard_map/all_gather | solution.py:52
  105.3 1.7 copy-start.1
  105.3 1.7 copy-start.4
  105.3 1.9 copy-start
  105.3 1.9 copy-start.3
  105.3 2.0 copy-start.2
  106.9 180.9 %all-gather.8.cloned.1.call-start = ((), (), s32[]{:S(2)}) async-start(), calls=%async_computation.4 | async-start | bytes 19464192 | tf_op jit(solution)/shard_map/all_gather | solution.py:69
  287.8 44.4 %slice-start = ((s8[18874368]{0:T(1024)(128)(4,1)}), s8[4194304]{0:T(1024)(128)(4,1)S(1)}, s32[]{:S(2)}) async-start(s8[18874368]{0:T(1024)(128)(4,1)} %bitcast.16), calls=%async_computation.5 | async-start | bytes 8388608
  287.8 44.4 %slice-start.1 = ((s8[18874368]{0:T(1024)(128)(4,1)}), s8[4194304]{0:T(1024)(128)(4,1)S(1)}, s32[]{:S(2)}) async-start(s8[18874368]{0:T(1024)(128)(4,1)} %bitcast.16), calls=%async_computation.6 | async-start | bytes 8388608
  287.8 44.5 %slice-start.2 = ((s8[18874368]{0:T(1024)(128)(4,1)}), s8[4194304]{0:T(1024)(128)(4,1)S(1)}, s32[]{:S(2)}) async-start(s8[18874368]{0:T(1024)(128)(4,1)} %bitcast.16), calls=%async_computation.7 | async-start | bytes 8388608
  287.8 44.5 %slice-start.3 = ((s8[18874368]{0:T(1024)(128)(4,1)}), s8[4194304]{0:T(1024)(128)(4,1)S(1)}, s32[]{:S(2)}) async-start(s8[18874368]{0:T(1024)(128)(4,1)} %bitcast.16), calls=%async_computation.8 | async-start | bytes 8388608
  299.3 32.9 %slice-start.4 = ((s8[18874368]{0:T(1024)(128)(4,1)}), s8[2097152]{0:T(1024)(128)(4,1)S(1)}, s32[]{:S(2)}) async-start(s8[18874368]{0:T(1024)(128)(4,1)} %bitcast.16), calls=%async_computation.9 | async-start | bytes 4194304
  331.9 1.3 copy-start.5
  331.9 1.6 copy-start.6
Sparse Core Ops, SparseCore 0:
  9.9 92.9 all-gather.3
  107.0 53.9 all-gather.5
  171.3 116.4 all-gather.7
where the time goes:
time: 346 us; the launch traced here: 345 us
  waiting for transfers between devices  224 us (65%)
  blocking collectives  63.7 us (18%)
  matrix products  23.9 us (7%)
  between operations  14.1 us (4%)
  other arithmetic  11.6 us (3%)
  local copies, waits for them, and re-layouts  7.24 us (2%)
    all_gather x1, waiting for transfers between devices, on_device(): panel_pairs = lax.all_gather(pair_density, 'col', axis=0, tiled=True)  94.8 us
    all_gather x1, waiting for transfers between devices, on_device(): panel_mixed = lax.all_gather(mixed_b, 'col', axis=1, tiled=True)  84 us
    all_to_all x2, blocking collectives, copy_for_each(): return lax.all_to_all(copies, axis, split_axis=0, concat_axis=0, tiled=True)  63.7 us
    all_gather x1, waiting for transfers between devices, on_device(): candidates = lax.all_gather(own_slice, 'row', axis=1, tiled=True)  44.8 us
    dot_general x1, matrix products, on_device(): jnp.dot(panel_mixed, strip_mixed, preferred_element_type=jnp.float32)  11.4 us
    dot_general x1, matrix products, on_device(): lax.dot_general(weighted, strip_pairs, (((0,), (0,)), ((), ())), preferre...  7.63 us
  transfers between devices with their start and end apart: 3, of which 3 were waited for; matrix products, arithmetic and copies ran while one was open for 3% of the time, Pallas kernels for 0%

commit v1 on v0

v1 whole, which is shorter than its diff:
```python
import functools
import math

import jax
import jax.numpy as jnp
from jax import lax
from jax.experimental import pallas as pl
from jax.experimental.pallas import tpu as pltpu
from jax.sharding import PartitionSpec as P


SHIFTS = (1, 3, 2)
LANES = 128
VMEM = pl.BlockSpec(memory_space=pltpu.VMEM)
SMEM = pl.BlockSpec(memory_space=pltpu.SMEM)
F32, BF16 = jnp.float32, jnp.bfloat16
shape = jax.ShapeDtypeStruct


def call(body, out_shape, operands, scratch=(), limit=4, scalars=(), flops=10**6):
    return pl.pallas_call(
        body,
        out_shape=out_shape,
        in_specs=[SMEM if i in scalars else VMEM for i in range(len(operands))],
        out_specs=jax.tree.map(lambda _: VMEM, out_shape),
        scratch_shapes=list(scratch),
        compiler_params=pltpu.CompilerParams(vmem_limit_bytes=limit << 20),
        cost_estimate=pl.CostEstimate(flops=flops, bytes_accessed=10**6, transcendentals=0),
    )(*operands)


def position():
    devices, count = lax.axis_size("col"), lax.axis_size("row")
    return lax.axis_index("col"), lax.axis_index("row"), devices, count


def setup_body(valence, conduction, momentum, bands, waves, scale, weight, sqrt_rows, sqrt_cols, scale_rows, scale_cols):
    column, here, _, _ = position()
    height, width = sqrt_rows.shape[1], sqrt_cols.shape[0]
    upper, lower = bands[0], bands[1]
    start = jnp.zeros(upper.shape, F32)
    valence_of = lax.fori_loop(0, valence.shape[0], lambda i, x: jnp.where(upper == i, valence[i], x), start, unroll=8)
    conduction_of = lax.fori_loop(0, conduction.shape[0], lambda i, x: jnp.where(lower == i, conduction[i], x), start)
    weight[...] = 4.0 / (valence_of - conduction_of)

    def root(at, size):
        total = None
        for i in range(waves.shape[0]):
            moved = waves[i : i + 1, pl.ds(at, size)].astype(F32) + momentum[i]
            total = moved * moved if total is None else total + moved * moved
        return jnp.sqrt(4.0 * math.pi / total)

    def turned(pair):
        one = jnp.where(column % 2 == 0, pair[:, :width], pair[:, width:])
        return jnp.broadcast_to(one, (LANES, width)).T

    first = pl.multiple_of(here * height, LANES)
    sqrt_rows[...] = root(first, height)
    scale_rows[...] = scale[:, pl.ds(first, height)]
    first = pl.multiple_of(column // 2 * (2 * width), LANES)
    sqrt_cols[...] = turned(root(first, 2 * width))
    scale_cols[...] = turned(scale[:, pl.ds(first, 2 * width)])


def factors(parts, weight, column, devices, rows):
    lane = lax.broadcasted_iota(jnp.int32, weight.shape, 1)
    core = column % 2
    found = []
    for steps, origin, first, size, _ in parts:
        chip = column - core + (4 * core - 2) * steps
        mine = lane == (chip + (core if origin is None else origin) + devices) % devices
        found.append(jnp.sum(jnp.where(mine, weight[...], 0.0), axis=1, keepdims=True)[first : first + size])
    return jnp.broadcast_to(jnp.concatenate(found, axis=0), (rows, LANES))


def weigh(at, block, factor, previous, weighted, turned, diagonal):
    wide = block.astype(F32)
    scaled = (factor * wide).astype(BF16)
    weighted[:, at] = scaled
    diagonal[:, at] = previous[:, at] + jnp.sum(scaled.astype(F32) * wide, axis=0, keepdims=True)
    turned[at, :] = block.T


def prepare_body(parts, weight, previous, *refs):
    pieces, (raw, turned, weighted, row, diagonal) = refs[: len(parts)], refs[len(parts) :]
    column, _, devices, _ = position()
    factor = factors(parts, weight, column, devices, weighted.shape[0])
    row[...] = factor.T[:1]

    def step(i, carry):
        at = pl.ds(pl.multiple_of(i * LANES, LANES), LANES)
        block = jnp.concatenate([r[f : f + n, at] for r, (*_, n, f) in zip(pieces, parts)], axis=0)
        raw[:, at] = block
        weigh(at, block, factor, previous, weighted, turned, diagonal)
        return carry

    lax.fori_loop(0, weighted.shape[1] // LANES, step, 0)


def finish_body(parts, weight, previous, raw, beside, turned, weighted, row, diagonal, strip):
    column, _, devices, _ = position()
    factor = factors(parts, weight, column + 1 - 2 * (column % 2), devices, weighted.shape[0])
    row[...] = factor.T[:1]

    def step(i, carry):
        at = pl.ds(pl.multiple_of(i * LANES, LANES), LANES)
        weigh(at, raw[:, at], factor, previous, weighted, turned, diagonal)
        return carry

    lax.fori_loop(0, weighted.shape[1] // LANES, step, 0)
    height, rows = strip.shape[0], raw.shape[0]
    first = pl.multiple_of((column * height) % turned.shape[0], 16)
    strip[:, :rows] = beside[pl.ds(first, height), :]
    strip[:, rows:] = turned[pl.ds(first, height), :]


def join_body(own, beside, out):
    column, _, _, _ = position()
    rows, core = own.shape[0], column % 2

    @pl.when(core == 0)
    def _():
        out[:rows], out[rows:] = own[...], beside[...]

    @pl.when(core == 1)
    def _():
        out[:rows], out[rows:] = beside[...], own[...]


def half_body(block, out):
    column, _, _, _ = position()
    rows = out.shape[0]
    out[...] = block[pl.ds(pl.multiple_of(column % 2 * rows, 16), rows), :]


def gate_body(token, out):
    out[...] = token[...]


def send_products(operand, turned, sends):
    size, at = sends.shape[2], 0
    for block in turned:
        rows = block.shape[1]
        first = at % size
        product = jnp.dot(operand[...], block[...], preferred_element_type=F32)
        sends[at // size, :, first : first + rows] = product.astype(BF16)
        at += rows


def unit_at(block_shape, first, height):
    column, here, _, _ = position()
    rows = lax.broadcasted_iota(jnp.int32, block_shape, 1) + (here * height + first)
    return rows == lax.broadcasted_iota(jnp.int32, block_shape, 0) + column * block_shape[0]


def summed(operand, weighted, at):
    total, first = None, 0
    for block in weighted:
        rows = block.shape[0]
        given = operand[:, first : first + rows] if len(operand.shape) == 2 else (
            operand[first // operand.shape[2], :, first % operand.shape[2] : first % operand.shape[2] + rows]
        )
        product = jnp.dot(given, block[:, at], preferred_element_type=F32)
        total = product if total is None else total + product
        first += rows
    return total


CHUNK = 256


def chunks(width, body):
    def step(i, carry):
        body(i * CHUNK, pl.ds(pl.multiple_of(i * CHUNK, CHUNK), CHUNK))
        return carry

    lax.fori_loop(0, width // CHUNK, step, 0)


def start_body(n, sqrt_rows, sqrt_cols, scale_rows, scale_cols, diagonal, token, *refs):
    strips, rows, refs = refs[: 4 * n], refs[4 * n : 6 * n], refs[6 * n :]
    weighted, turned, refs = refs[: 2 * n], refs[2 * n : 4 * n], refs[4 * n :]
    epsilon, mixed, guess_rows, sends, chosen, operand, line = refs
    column, here, _, count = position()
    width, height = mixed.shape
    relative = (here + count - (column * width) // height) % count
    at = 0
    for i in range(n):
        size = strips[4 * i].shape[1]
        for j in range(4):

            @pl.when(relative == j)
            def _():
                chosen[:, at : at + size] = strips[4 * i + j][...]

        at += size
    at = 0
    for row in rows:
        line[:, at : at + row.shape[1]] = row[...]
        at += row.shape[1]

    def add(i, total):
        lanes = pl.ds(pl.multiple_of(i * LANES, LANES), LANES)
        wide = chosen[:, lanes].astype(F32)
        return total + (line[:, lanes] * wide).astype(BF16).astype(F32) * wide

    total = lax.fori_loop(0, chosen.shape[1] // LANES, add, jnp.zeros((width, LANES), F32))
    chi_cols = jnp.sum(total, axis=1, keepdims=True)
    s_cols = sqrt_cols[:, :1]
    g_cols = scale_cols[:, :1] / (1.0 - s_cols * chi_cols * s_cols)
    s_all = sqrt_rows[...]
    guess_rows[...] = scale_rows[...] / (1.0 - s_all * diagonal[...] * s_all)

    def part(first, at):
        s_rows, g_rows = sqrt_rows[:, at], guess_rows[:, at]
        block = jnp.where(unit_at((width, CHUNK), first, height), 1.0, 0.0) - s_cols * summed(chosen, weighted, at) * s_rows
        epsilon[:, at] = block
        found = block * g_cols
        mixed[:, at] = found
        operand[:, at] = (s_rows * (g_rows * found.astype(BF16).astype(F32))).astype(BF16)

    chunks(height, part)
    send_products(operand, turned, sends)


def combine_body(parts, out):
    total = parts[0].astype(F32)
    for i in range(1, parts.shape[0]):
        total += parts[i].astype(F32)
    total = total.astype(BF16)
    for i in range(parts.shape[0]):
        out[i] = total


def middle_body(n, sqrt_rows, guess_rows, mixed, *refs):
    filled, *refs = refs
    weighted, turned, refs = refs[:n], refs[n : 2 * n], refs[2 * n :]
    square, sends, operand = refs

    def part(first, at):
        s_rows, g_rows = sqrt_rows[:, at], guess_rows[:, at]
        value = g_rows * mixed[:, at].astype(BF16).astype(F32) - s_rows * summed(filled, weighted, at)
        square[:, at] = value
        operand[:, at] = (s_rows * (g_rows * value.astype(BF16).astype(F32))).astype(BF16)

    chunks(mixed.shape[1], part)
    send_products(operand, turned, sends)


def final_body(sqrt_rows, guess_rows, mixed, square, *refs):
    filled, weighted, inverse = refs[0], refs[1:-1], refs[-1]
    width, height = mixed.shape

    def part(first, at):
        s_rows, g_rows, s = sqrt_rows[:, at], guess_rows[:, at], square[:, at]
        cube = g_rows * s.astype(BF16).astype(F32) - s_rows * summed(filled, weighted, at)
        unit = jnp.where(unit_at((width, CHUNK), first, height), 4.0, 0.0)
        inverse[:, at] = g_rows * (unit - 6.0 * mixed[:, at] + 4.0 * s - cube)

    chunks(height, part)


def on_device(pair_density, band_pairs, valence, conduction, wave_vectors, momentum, guess_scale):
    devices, count = lax.axis_size("col"), lax.axis_size("row")
    own_pairs, height = pair_density.shape
    width = height * count // devices
    pairs = own_pairs * devices
    sibling = [(c, c ^ 1) for c in range(devices)]
    last = devices // 4

    def shifted(array, shift):
        return lax.ppermute(array, "row", [(r, (r + shift) % count) for r in range(count)])

    beside = lax.ppermute(pair_density, "col", sibling)
    ring = [call(join_body, shape((2 * own_pairs, height), BF16), [pair_density, beside])]
    onward = [(c, (c + 2 - 4 * (c % 2)) % devices) for c in range(devices)]
    token = jnp.zeros((8, LANES), F32)
    for step in range(1, last + 1):
        block = ring[-1]
        if step == last:
            block = call(half_body, shape((own_pairs, height), BF16), [block])
        ring.append(lax.ppermute(block, "col", onward))
        token = call(gate_body, shape(token.shape, F32), [token])

    bands = band_pairs.reshape(2, devices, own_pairs).transpose(0, 2, 1)
    weight, sqrt_rows, sqrt_cols, scale_rows, scale_cols = call(
        setup_body,
        (
            shape((own_pairs, devices), F32),
            shape((1, height), F32),
            shape((width, LANES), F32),
            shape((1, height), F32),
            shape((width, LANES), F32),
        ),
        [valence, conduction, momentum, bands, wave_vectors, guess_scale[None, :]],
        scalars=(0, 1, 2),
    )
    turned, weighted, rows, strips = [], [], [], []
    diagonal = jnp.zeros((1, height), F32)

    def group(parts, pieces):
        nonlocal diagonal
        size, row = sum(part[3] for part in parts), shape((1, height), F32)
        made = (shape((height, size), BF16), shape((size, height), BF16), shape((1, size), F32), row)
        raw, t, w, line, diagonal = call(
            functools.partial(prepare_body, parts), (shape((size, height), BF16), *made), [weight, diagonal, *pieces]
        )
        raw = lax.ppermute(raw, "col", sibling)
        turn, weigh, row, diagonal, strip = call(
            functools.partial(finish_body, parts), (*made, shape((width, 2 * size), BF16)), [weight, diagonal, raw, t]
        )
        above, below, far = (shifted(strip, shift) for shift in SHIFTS)
        strips.extend([strip, above, far, below])
        rows.extend([line, row])
        turned.extend([t, turn])
        weighted.extend([w, weigh])

    def whole(*steps):
        return tuple((step, core, 0, own_pairs, core * own_pairs) for step in steps for core in range(2))

    def pieces_of(*steps):
        return [ring[step] for step in steps for _ in range(2)]

    rest = 2 * own_pairs // 3
    for first in (1, 3, 5):
        group(whole(first, first + 1), pieces_of(first, first + 1))
    group(whole(last - 1) + ((0, None, 0, rest, 0),), pieces_of(last - 1) + [pair_density])
    group(((0, None, rest, own_pairs - rest, rest), (last, None, 0, own_pairs, 0)), [pair_density, ring[last]])

    n = len(strips) // 4

    size = pairs // count
    tall, flat = (width, size), (width, height)
    traded = shape((count, *tall), BF16)
    filled = pltpu.VMEM((width, pairs), BF16)
    operand = pltpu.VMEM(flat, BF16)

    def swapped(array):
        return lax.all_to_all(array, "row", split_axis=0, concat_axis=0, tiled=True)

    def exchange(sends):
        return swapped(call(combine_body, shape((count, *tall), BF16), [swapped(sends)]))

    epsilon, mixed, guess_rows, sends = call(
        functools.partial(start_body, n),
        (shape(flat, F32), shape(flat, F32), shape((1, height), F32), traded),
        [sqrt_rows, sqrt_cols, scale_rows, scale_cols, diagonal, token, *strips, *rows, *weighted, *turned],
        [filled, operand, pltpu.VMEM((1, pairs), F32)],
        limit=12,
    )
    pieces = exchange(sends)
    square, sends = call(
        functools.partial(middle_body, 2 * n),
        (shape(flat, F32), traded),
        [sqrt_rows, guess_rows, mixed, pieces, *weighted, *turned],
        [operand],
        limit=12,
    )
    pieces = exchange(sends)
    inverse = call(final_body, shape(flat, F32), [sqrt_rows, guess_rows, mixed, square, pieces, *weighted], limit=12)
    return (epsilon.T, inverse.T)


def solution(mesh):
    placed = (P(("pb", "col"), "row"), P(), P(), P(), P(None, "pb"), P("pb"), P("pb"))

    return jax.shard_map(
        on_device,
        mesh=mesh,
        in_specs=placed,
        out_specs=(P(("pb", "row"), "col"), P(("pb", "row"), "col")),
        check_vma=False,
    )
```

time: 346 us -> 257 us (0.74)
  waiting for transfers between devices: 224 us -> 85.1 us
  starting transfers between devices: 0.19 us -> 63.7 us
  Pallas kernels: 0 us -> 34.1 us
  matrix products: 23.9 us -> 0 us
  between operations: 14.1 us -> 0.94 us
  other arithmetic: 11.6 us -> 0 us
  local copies, waits for them, and re-layouts: 7.24 us -> 1.18 us
  blocking collectives: 63.7 us -> 68.1 us
    all_gather x3 -> x0, waiting for transfers between devices: 224 us -> none  [the longest x1 94.8 us: on_device(): panel_pairs = lax.all_gather(pair_density, 'col', axis=0, tiled=True)]
    ppermute x0 -> x29, waiting for transfers between devices: none -> 85.1 us  [the longest x8 48.4 us: on_device(): ring.append(lax.ppermute(block, 'col', onward))]
    ppermute x0 -> x29, starting transfers between devices: none -> 63.7 us  [the longest x1 20.5 us: on_device(): beside = lax.ppermute(pair_density, 'col', sibling)]
    pallas_call x0 -> x26, Pallas kernels: none -> 34.1 us  [call(): pl.pallas_call(body, out_shape=out_shape, in_specs=[SMEM if i in scalars...]
    dot_general x3 -> x0, matrix products: 23.9 us -> none  [the longest x1 11.4 us: on_device(): jnp.dot(panel_mixed, strip_mixed, preferred_element_type=jnp.float32)]
    reduce_sum x5 -> x0, other arithmetic: 10 us -> none  [the longest x1 6.22 us: on_device(): jnp.sum(weighted.astype(jnp.float32) * panel_pairs.astype(jnp.float32), a...]
    all_to_all x2 -> x4, blocking collectives: 63.7 us -> 68.1 us  [swapped(): return lax.all_to_all(array, 'row', split_axis=0, concat_axis=0, tiled=True)]
    dynamic_slice x2 -> x0, local copies, waits for them, and re-layouts: 3.91 us -> none  [on_device(): own_slice = lax.dynamic_slice_in_dim(panel_pairs, offset, strip_width, 1)]
  transfers between devices with their start and end apart: 3 -> 29, of which waited for: 3 -> 17; matrix products, arithmetic and copies ran while one was open for 3% -> 0% of each run, Pallas kernels for 0% -> 4%
where the time goes in v1:
time: 257 us; the launch traced here: 253 us
  waiting for transfers between devices  85.1 us (33%)
  blocking collectives  68.1 us (26%)
  starting transfers between devices  63.7 us (25%)
  Pallas kernels  34.1 us (13%)
    all_to_all x4, blocking collectives, swapped(): return lax.all_to_all(array, 'row', split_axis=0, concat_axis=0, tiled=True)  68.1 us
    ppermute x8, waiting for transfers between devices, on_device(): ring.append(lax.ppermute(block, 'col', onward))  48.4 us
    pallas_call x26, Pallas kernels, call(): pl.pallas_call(body, out_shape=out_shape, in_specs=[SMEM if i in scalars...  34.1 us
    ppermute x15, waiting for transfers between devices, shifted(): lax.ppermute(array, 'row', [(r, (r + shift) % count) for r in range(count)])  32.8 us
    ppermute x1, starting transfers between devices, on_device(): beside = lax.ppermute(pair_density, 'col', sibling)  20.5 us
    ppermute x15, starting transfers between devices, shifted(): lax.ppermute(array, 'row', [(r, (r + shift) % count) for r in range(count)])  18.2 us
    ppermute x5, starting transfers between devices, group(): raw = lax.ppermute(raw, 'col', sibling)  15.6 us
    ppermute x8, starting transfers between devices, on_device(): ring.append(lax.ppermute(block, 'col', onward))  9.34 us
  transfers between devices with their start and end apart: 29, of which 17 were waited for; matrix products, arithmetic and copies ran while one was open for 0% of the time, Pallas kernels for 4%

profile of v1, /device:TPU:33, one launch (start us, length us, event | category | flops | bytes accessed | tf_op | source)
XLA Modules:
  0.0 253.2 jit_solution(4576693184191521232)
XLA Ops:
  0.6 20.5 %collective-permute-start = (bf16[96,1536]{1,0:T(8,128)(2,1)}, bf16[96,1536]{1,0:T(8,128)(2,1)S(1)}, u32[]{:S(2)}, u32[]{:S(2)}) collective-permute-start(bf16[96,1536]{1,0:T(8,128)(2,1)} %refs_0_.1), channel_id=1, source_target_pairs={{0,4},{4,0},{8,12},{12,8},{16,20},{20,16},{24,28},{28,24},{32,36},... | collective-permute-start | bytes 884744 | tf_op jit(solution)/shard_map/ppermute | solution.py:274
  23.6 3.2 %collective-permute-start.1 = (bf16[192,1536]{1,0:T(8,128)(2,1)S(1)}, bf16[192,1536]{1,0:T(8,128)(2,1)S(1)}, u32[]{:S(2)}, u32[]{:S(2)}) collective-permute-start(bf16[192,1536]{1,0:T(8,128)(2,1)S(1)} %shard_map.87), channel_id=1, source_target_pairs={{0,8},{4,124},{8,16},{12,4},{16,24},{20,12},{24,32},{28,20},{32,40... | collective-permute-start | bytes 1769480 | tf_op jit(solution)/shard_map/ppermute | solution.py:282
  26.9 6.8 %collective-permute-done.1.refs_0_.refs_1_ = bf16[192,1536]{1,0:T(8,128)(2,1)S(1)} collective-permute-done((bf16[192,1536]{1,0:T(8,128)(2,1)S(1)}, bf16[192,1536]{1,0:T(8,128)(2,1)S(1)}, u32[]{:S(2)}, u32[]{:S(2)}) %collective-permute-start.1) | collective-permute-done | bytes 589856 | tf_op jit(solution)/shard_map/ppermute | solution.py:282
  39.0 4.7 %collective-permute-done.2.refs_2_.refs_3_ = bf16[192,1536]{1,0:T(8,128)(2,1)S(1)} collective-permute-done((bf16[192,1536]{1,0:T(8,128)(2,1)S(1)}, bf16[192,1536]{1,0:T(8,128)(2,1)S(1)}, u32[]{:S(2)}, u32[]{:S(2)}) %collective-permute-start.2) | collective-permute-done | bytes 589856 | tf_op jit(solution)/shard_map/ppermute | solution.py:282
  48.7 8.5 %collective-permute-done.4.refs_0_.refs_1_ = bf16[192,1536]{1,0:T(8,128)(2,1)S(1)} collective-permute-done((bf16[192,1536]{1,0:T(8,128)(2,1)S(1)}, bf16[192,1536]{1,0:T(8,128)(2,1)S(1)}, u32[]{:S(2)}, u32[]{:S(2)}) %collective-permute-start.4) | collective-permute-done | bytes 589856 | tf_op jit(solution)/shard_map/ppermute | solution.py:282
  60.1 6.1 %collective-permute-done.5.refs_2_.refs_3_ = bf16[192,1536]{1,0:T(8,128)(2,1)S(1)} collective-permute-done((bf16[192,1536]{1,0:T(8,128)(2,1)S(1)}, bf16[192,1536]{1,0:T(8,128)(2,1)S(1)}, u32[]{:S(2)}, u32[]{:S(2)}) %collective-permute-start.5) | collective-permute-done | bytes 589856 | tf_op jit(solution)/shard_map/ppermute | solution.py:282
  67.8 4.4 %collective-permute-start.6 = (bf16[384,1536]{1,0:T(8,128)(2,1)S(1)}, bf16[384,1536]{1,0:T(8,128)(2,1)S(1)}, u32[]{:S(2)}, u32[]{:S(2)}) collective-permute-start(bf16[384,1536]{1,0:T(8,128)(2,1)S(1)} %get-tuple-element.73), channel_id=1, source_target_pairs={{0,4},{4,0},{8,12},{12,8},{16,20},{20,16},{24,28},{28,24},{32,36},... | collective-permute-start | bytes 3538952 | tf_op jit(solution)/shard_map/ppermute | solution.py:308
  72.2 9.0 %collective-permute-done.7.refs_0_.refs_1_ = bf16[192,1536]{1,0:T(8,128)(2,1)S(1)} collective-permute-done((bf16[192,1536]{1,0:T(8,128)(2,1)S(1)}, bf16[192,1536]{1,0:T(8,128)(2,1)S(1)}, u32[]{:S(2)}, u32[]{:S(2)}) %collective-permute-start.7) | collective-permute-done | bytes 589856 | tf_op jit(solution)/shard_map/ppermute | solution.py:282
  83.6 6.6 %collective-permute-done.8.refs_2_.refs_3_ = bf16[192,1536]{1,0:T(8,128)(2,1)S(1)} collective-permute-done((bf16[192,1536]{1,0:T(8,128)(2,1)S(1)}, bf16[192,1536]{1,0:T(8,128)(2,1)S(1)}, u32[]{:S(2)}, u32[]{:S(2)}) %collective-permute-start.8) | collective-permute-done | bytes 589856 | tf_op jit(solution)/shard_map/ppermute | solution.py:282
  91.7 4.4 %collective-permute-start.9 = (bf16[384,1536]{1,0:T(8,128)(2,1)S(1)}, bf16[384,1536]{1,0:T(8,128)(2,1)S(1)}, u32[]{:S(2)}, u32[]{:S(2)}) collective-permute-start(bf16[384,1536]{1,0:T(8,128)(2,1)S(1)} %get-tuple-element.77), channel_id=1, source_target_pairs={{0,4},{4,0},{8,12},{12,8},{16,20},{20,16},{24,28},{28,24},{32,36},... | collective-permute-start | bytes 3538952 | tf_op jit(solution)/shard_map/ppermute | solution.py:308
  100.1 5.0 %collective-permute-done.10.refs_0_.refs_1_.block = bf16[192,1536]{1,0:T(8,128)(2,1)S(1)} collective-permute-done((bf16[192,1536]{1,0:T(8,128)(2,1)S(1)}, bf16[192,1536]{1,0:T(8,128)(2,1)S(1)}, u32[]{:S(2)}, u32[]{:S(2)}) %collective-permute-start.10) | collective-permute-done | bytes 589856 | tf_op jit(solution)/shard_map/ppermute | solution.py:282
  120.3 4.3 %collective-permute-done.16.refs_3_ = bf16[192,768]{1,0:T(8,128)(2,1)S(1)} collective-permute-done((bf16[192,768]{1,0:T(8,128)(2,1)S(1)}, bf16[192,768]{1,0:T(8,128)(2,1)S(1)}, u32[]{:S(2)}, u32[]{:S(2)}) %collective-permute-start.16) | collective-permute-done | bytes 294944 | tf_op jit(solution)/shard_map/ppermute | solution.py:272
  129.7 7.6 %collective-permute-done.19.refs_7_ = bf16[192,768]{1,0:T(8,128)(2,1)S(1)} collective-permute-done((bf16[192,768]{1,0:T(8,128)(2,1)S(1)}, bf16[192,768]{1,0:T(8,128)(2,1)S(1)}, u32[]{:S(2)}, u32[]{:S(2)}) %collective-permute-start.19) | collective-permute-done | bytes 294944 | tf_op jit(solution)/shard_map/ppermute | solution.py:272
  137.2 4.1 %collective-permute-start.20 = (bf16[192,768]{1,0:T(8,128)(2,1)S(1)}, bf16[192,768]{1,0:T(8,128)(2,1)S(1)}, u32[]{:S(2)}, u32[]{:S(2)}) collective-permute-start(bf16[192,768]{1,0:T(8,128)(2,1)S(1)} %get-tuple-element.90.refs_8_), channel_id=1, source_target_pairs={{0,1},{1,2},{2,3},{3,0},{4,5},{5,6},{6,7},{7,4},{8,9},{9,10},{10,1... | collective-permute-start | bytes 884744 | tf_op jit(solution)/shard_map/ppermute | solution.py:272
  141.8 7.9 %collective-permute-done.22.refs_11_ = bf16[192,768]{1,0:T(8,128)(2,1)S(1)} collective-permute-done((bf16[192,768]{1,0:T(8,128)(2,1)S(1)}, bf16[192,768]{1,0:T(8,128)(2,1)S(1)}, u32[]{:S(2)}, u32[]{:S(2)}) %collective-permute-start.22) | collective-permute-done | bytes 294944 | tf_op jit(solution)/shard_map/ppermute | solution.py:272
  149.7 4.3 %collective-permute-start.23 = (bf16[192,512]{1,0:T(8,128)(2,1)S(1)}, bf16[192,512]{1,0:T(8,128)(2,1)S(1)}, u32[]{:S(2)}, u32[]{:S(2)}) collective-permute-start(bf16[192,512]{1,0:T(8,128)(2,1)S(1)} %get-tuple-element.91.refs_12_), channel_id=1, source_target_pairs={{0,1},{1,2},{2,3},{3,0},{4,5},{5,6},{6,7},{7,4},{8,9},{9,10},{10,1... | collective-permute-start | bytes 589832 | tf_op jit(solution)/shard_map/ppermute | solution.py:272
  157.2 6.5 %collective-permute-done.23.refs_13_ = bf16[192,512]{1,0:T(8,128)(2,1)S(1)} collective-permute-done((bf16[192,512]{1,0:T(8,128)(2,1)S(1)}, bf16[192,512]{1,0:T(8,128)(2,1)S(1)}, u32[]{:S(2)}, u32[]{:S(2)}) %collective-permute-start.23) | collective-permute-done | bytes 196640 | tf_op jit(solution)/shard_map/ppermute | solution.py:272
  166.8 7.5 %shard_map.107 = (f32[192,1536]{1,0:T(8,128)}, f32[192,1536]{1,0:T(8,128)S(1)}, f32[1,1536]{1,0:T(1,128)S(1)}, bf16[4,192,768]{2,1,0:T(8,128)(2,1)S(1)}) custom-call(f32[1,1536]{1,0:T(1,128)S(1)} %get-tuple-element.63.sqrt_rows, f32[192,128]{1,0:T(8,128)S(1)} %get-tuple-element.64.sqrt_cols, f32[1,1536]{1,0:T(1,128)S(1)} %get-tuple-element.65.scale_rows, ...), custom_call_target="tpu_custom_call" | custom-call | flops 1000000 | bytes 1000000 | tf_op jit(solution)/shard_map/pallas_call | solution.py:21
  174.4 18.5 %all_to_all.20.parts = bf16[4,192,768]{2,1,0:T(8,128)(2,1)S(1)} all-to-all(bf16[4,192,768]{2,1,0:T(8,128)(2,1)S(1)} %get-tuple-element.121), channel_id=1, replica_groups=mesh['pb'=2,'col'=32,'row'=4] {'row'}, dimensions={0} | all-to-all | bytes 2359296 | tf_op jit(solution)/shard_map/all_to_all | solution.py:339
  193.0 17.4 %all_to_all.21.refs_0_ = bf16[4,192,768]{2,1,0:T(8,128)(2,1)S(1)} all-to-all(bf16[4,192,768]{2,1,0:T(8,128)(2,1)S(1)} %shard_map.108), channel_id=1, replica_groups=mesh['pb'=2,'col'=32,'row'=4] {'row'}, dimensions={0} | all-to-all | bytes 2359296 | tf_op jit(solution)/shard_map/all_to_all | solution.py:339
  210.4 6.1 %shard_map.109 = (f32[192,1536]{1,0:T(8,128)S(1)}, bf16[4,192,768]{2,1,0:T(8,128)(2,1)S(1)}) custom-call(f32[1,1536]{1,0:T(1,128)S(1)} %get-tuple-element.63.sqrt_rows, f32[1,1536]{1,0:T(1,128)S(1)} %get-tuple-element.119.guess_rows, f32[192,1536]{1,0:T(8,128)S(1)} %get-tuple-element.120.mixed, bf16[4,192,768]{2,1,0:T(8,128)(2,1)S(1)} %all_to_all.21.refs_0_, ...), custom_call_target="tpu_custom_call" | custom-call | flops 1000000 | bytes 1000000 | tf_op jit(solution)/shard_map/pallas_call | solution.py:21
  216.5 16.5 %all_to_all.22.parts = bf16[4,192,768]{2,1,0:T(8,128)(2,1)S(1)} all-to-all(bf16[4,192,768]{2,1,0:T(8,128)(2,1)S(1)} %get-tuple-element.123), channel_id=1, replica_groups=mesh['pb'=2,'col'=32,'row'=4] {'row'}, dimensions={0} | all-to-all | bytes 2359296 | tf_op jit(solution)/shard_map/all_to_all | solution.py:339
  233.1 15.7 %all_to_all.23.refs_0_ = bf16[4,192,768]{2,1,0:T(8,128)(2,1)S(1)} all-to-all(bf16[4,192,768]{2,1,0:T(8,128)(2,1)S(1)} %shard_map.110), channel_id=1, replica_groups=mesh['pb'=2,'col'=32,'row'=4] {'row'}, dimensions={0} | all-to-all | bytes 2359296 | tf_op jit(solution)/shard_map/all_to_all | solution.py:339
  248.8 4.4 %shard_map.111 = f32[192,1536]{1,0:T(8,128)} custom-call(f32[1,1536]{1,0:T(1,128)S(1)} %get-tuple-element.63.sqrt_rows, f32[1,1536]{1,0:T(1,128)S(1)} %get-tuple-element.119.guess_rows, f32[192,1536]{1,0:T(8,128)S(1)} %get-tuple-element.120.mixed, f32[192,1536]{1,0:T(8,128)S(1)} %get-tuple-element.122.square, bf16[4,192,768]{2,1,0:T(8,128)(2,1)S(1)} %all_to_all.23.refs_0_, ...), custom_call_target="tpu_custom_call" | custom-call | flops 1000000 | bytes 1000000 | tf_op jit(solution)/shard_map/pallas_call | solution.py:21
  (84 shorter events, 52.2 us)
Async XLA Ops:
  0.6 22.0 %collective-permute-start = (bf16[96,1536]{1,0:T(8,128)(2,1)}, bf16[96,1536]{1,0:T(8,128)(2,1)S(1)}, u32[]{:S(2)}, u32[]{:S(2)}) collective-permute-start(bf16[96,1536]{1,0:T(8,128)(2,1)} %refs_0_.1), channel_id=1, source_target_pairs={{0,4},{4,0},{8,12},{12,8},{16,20},{20,16},{24,28},{28,24},{32,36},... | collective-permute-start | bytes 884744 | tf_op jit(solution)/shard_map/ppermute | solution.py:274
  23.6 10.1 %collective-permute-start.1 = (bf16[192,1536]{1,0:T(8,128)(2,1)S(1)}, bf16[192,1536]{1,0:T(8,128)(2,1)S(1)}, u32[]{:S(2)}, u32[]{:S(2)}) collective-permute-start(bf16[192,1536]{1,0:T(8,128)(2,1)S(1)} %shard_map.87), channel_id=1, source_target_pairs={{0,8},{4,124},{8,16},{12,4},{16,24},{20,12},{24,32},{28,20},{32,40... | collective-permute-start | bytes 1769480 | tf_op jit(solution)/shard_map/ppermute | solution.py:282
  33.7 9.9 %collective-permute-start.2 = (bf16[192,1536]{1,0:T(8,128)(2,1)S(1)}, bf16[192,1536]{1,0:T(8,128)(2,1)S(1)}, u32[]{:S(2)}, u32[]{:S(2)}) collective-permute-start(bf16[192,1536]{1,0:T(8,128)(2,1)S(1)} %collective-permute-done.1.refs_0_.refs_1_), channel_id=1, source_target_pairs={{0,8},{4,124},{8,16},{12,4},{16,24},{20,12},{24,32},{28,20},{32,40... | collective-permute-start | bytes 1769480 | tf_op jit(solution)/shard_map/ppermute | solution.py:282
  45.2 13.4 %collective-permute-start.3 = (bf16[384,1536]{1,0:T(8,128)(2,1)S(1)}, bf16[384,1536]{1,0:T(8,128)(2,1)S(1)}, u32[]{:S(2)}, u32[]{:S(2)}) collective-permute-start(bf16[384,1536]{1,0:T(8,128)(2,1)S(1)} %get-tuple-element.69), channel_id=1, source_target_pairs={{0,4},{4,0},{8,12},{12,8},{16,20},{20,16},{24,28},{28,24},{32,36},... | collective-permute-start | bytes 3538952 | tf_op jit(solution)/shard_map/ppermute | solution.py:308
  48.1 9.0 %collective-permute-start.4 = (bf16[192,1536]{1,0:T(8,128)(2,1)S(1)}, bf16[192,1536]{1,0:T(8,128)(2,1)S(1)}, u32[]{:S(2)}, u32[]{:S(2)}) collective-permute-start(bf16[192,1536]{1,0:T(8,128)(2,1)S(1)} %collective-permute-done.2.refs_2_.refs_3_), channel_id=1, source_target_pairs={{0,8},{4,124},{8,16},{12,4},{16,24},{20,12},{24,32},{28,20},{32,40... | collective-permute-start | bytes 1769480 | tf_op jit(solution)/shard_map/ppermute | solution.py:282
  57.2 9.0 %collective-permute-start.5 = (bf16[192,1536]{1,0:T(8,128)(2,1)S(1)}, bf16[192,1536]{1,0:T(8,128)(2,1)S(1)}, u32[]{:S(2)}, u32[]{:S(2)}) collective-permute-start(bf16[192,1536]{1,0:T(8,128)(2,1)S(1)} %collective-permute-done.4.refs_0_.refs_1_), channel_id=1, source_target_pairs={{0,8},{4,124},{8,16},{12,4},{16,24},{20,12},{24,32},{28,20},{32,40... | collective-permute-start | bytes 1769480 | tf_op jit(solution)/shard_map/ppermute | solution.py:282
  67.8 14.3 %collective-permute-start.6 = (bf16[384,1536]{1,0:T(8,128)(2,1)S(1)}, bf16[384,1536]{1,0:T(8,128)(2,1)S(1)}, u32[]{:S(2)}, u32[]{:S(2)}) collective-permute-start(bf16[384,1536]{1,0:T(8,128)(2,1)S(1)} %get-tuple-element.73), channel_id=1, source_target_pairs={{0,4},{4,0},{8,12},{12,8},{16,20},{20,16},{24,28},{28,24},{32,36},... | collective-permute-start | bytes 3538952 | tf_op jit(solution)/shard_map/ppermute | solution.py:308
  72.1 9.0 %collective-permute-start.7 = (bf16[192,1536]{1,0:T(8,128)(2,1)S(1)}, bf16[192,1536]{1,0:T(8,128)(2,1)S(1)}, u32[]{:S(2)}, u32[]{:S(2)}) collective-permute-start(bf16[192,1536]{1,0:T(8,128)(2,1)S(1)} %collective-permute-done.5.refs_2_.refs_3_), channel_id=1, source_target_pairs={{0,8},{4,124},{8,16},{12,4},{16,24},{20,12},{24,32},{28,20},{32,40... | collective-permute-start | bytes 1769480 | tf_op jit(solution)/shard_map/ppermute | solution.py:282
  81.2 9.0 %collective-permute-start.8 = (bf16[192,1536]{1,0:T(8,128)(2,1)S(1)}, bf16[192,1536]{1,0:T(8,128)(2,1)S(1)}, u32[]{:S(2)}, u32[]{:S(2)}) collective-permute-start(bf16[192,1536]{1,0:T(8,128)(2,1)S(1)} %collective-permute-done.7.refs_0_.refs_1_), channel_id=1, source_target_pairs={{0,8},{4,124},{8,16},{12,4},{16,24},{20,12},{24,32},{28,20},{32,40... | collective-permute-start | bytes 1769480 | tf_op jit(solution)/shard_map/ppermute | solution.py:282
  96.1 9.0 %collective-permute-start.10 = (bf16[192,1536]{1,0:T(8,128)(2,1)S(1)}, bf16[192,1536]{1,0:T(8,128)(2,1)S(1)}, u32[]{:S(2)}, u32[]{:S(2)}) collective-permute-start(bf16[192,1536]{1,0:T(8,128)(2,1)S(1)} %collective-permute-done.8.refs_2_.refs_3_), channel_id=1, source_target_pairs={{0,8},{4,124},{8,16},{12,4},{16,24},{20,12},{24,32},{28,20},{32,40... | collective-permute-start | bytes 1769480 | tf_op jit(solution)/shard_map/ppermute | solution.py:282
  106.4 11.2 %collective-permute-start.11 = (bf16[256,1536]{1,0:T(8,128)(2,1)S(1)}, bf16[256,1536]{1,0:T(8,128)(2,1)S(1)}, u32[]{:S(2)}, u32[]{:S(2)}) collective-permute-start(bf16[256,1536]{1,0:T(8,128)(2,1)S(1)} %get-tuple-element.81), channel_id=1, source_target_pairs={{0,4},{4,0},{8,12},{12,8},{16,20},{20,16},{24,28},{28,24},{32,36},... | collective-permute-start | bytes 2359304 | tf_op jit(solution)/shard_map/ppermute | solution.py:308
  108.9 15.7 %collective-permute-start.16 = (bf16[192,768]{1,0:T(8,128)(2,1)S(1)}, bf16[192,768]{1,0:T(8,128)(2,1)S(1)}, u32[]{:S(2)}, u32[]{:S(2)}) collective-permute-start(bf16[192,768]{1,0:T(8,128)(2,1)S(1)} %get-tuple-element.88.refs_0_), channel_id=1, source_target_pairs={{0,3},{1,0},{2,1},{3,2},{4,7},{5,4},{6,5},{7,6},{8,11},{9,8},{10,9... | collective-permute-start | bytes 884744 | tf_op jit(solution)/shard_map/ppermute | solution.py:272
  112.1 14.1 %collective-permute-start.15 = (bf16[192,768]{1,0:T(8,128)(2,1)S(1)}, bf16[192,768]{1,0:T(8,128)(2,1)S(1)}, u32[]{:S(2)}, u32[]{:S(2)}) collective-permute-start(bf16[192,768]{1,0:T(8,128)(2,1)S(1)} %get-tuple-element.88.refs_0_), channel_id=1, source_target_pairs={{0,2},{1,3},{2,0},{3,1},{4,6},{5,7},{6,4},{7,5},{8,10},{9,11},{10,... | collective-permute-start | bytes 884744 | tf_op jit(solution)/shard_map/ppermute | solution.py:272
  112.4 17.1 %collective-permute-start.14 = (bf16[192,768]{1,0:T(8,128)(2,1)S(1)}, bf16[192,768]{1,0:T(8,128)(2,1)S(1)}, u32[]{:S(2)}, u32[]{:S(2)}) collective-permute-start(bf16[192,768]{1,0:T(8,128)(2,1)S(1)} %get-tuple-element.88.refs_0_), channel_id=1, source_target_pairs={{0,1},{1,2},{2,3},{3,0},{4,5},{5,6},{6,7},{7,4},{8,9},{9,10},{10,1... | collective-permute-start | bytes 884744 | tf_op jit(solution)/shard_map/ppermute | solution.py:272
  114.8 22.5 %collective-permute-start.19 = (bf16[192,768]{1,0:T(8,128)(2,1)S(1)}, bf16[192,768]{1,0:T(8,128)(2,1)S(1)}, u32[]{:S(2)}, u32[]{:S(2)}) collective-permute-start(bf16[192,768]{1,0:T(8,128)(2,1)S(1)} %get-tuple-element.89.refs_4_), channel_id=1, source_target_pairs={{0,3},{1,0},{2,1},{3,2},{4,7},{5,4},{6,5},{7,6},{8,11},{9,8},{10,9... | collective-permute-start | bytes 884744 | tf_op jit(solution)/shard_map/ppermute | solution.py:272
  117.7 19.6 %collective-permute-start.18 = (bf16[192,768]{1,0:T(8,128)(2,1)S(1)}, bf16[192,768]{1,0:T(8,128)(2,1)S(1)}, u32[]{:S(2)}, u32[]{:S(2)}) collective-permute-start(bf16[192,768]{1,0:T(8,128)(2,1)S(1)} %get-tuple-element.89.refs_4_), channel_id=1, source_target_pairs={{0,2},{1,3},{2,0},{3,1},{4,6},{5,7},{6,4},{7,5},{8,10},{9,11},{10,... | collective-permute-start | bytes 884744 | tf_op jit(solution)/shard_map/ppermute | solution.py:272
  124.6 25.1 %collective-permute-start.13 = (bf16[128,1536]{1,0:T(8,128)(2,1)S(1)}, bf16[128,1536]{1,0:T(8,128)(2,1)S(1)}, u32[]{:S(2)}, u32[]{:S(2)}) collective-permute-start(bf16[128,1536]{1,0:T(8,128)(2,1)S(1)} %get-tuple-element.85), channel_id=1, source_target_pairs={{0,4},{4,0},{8,12},{12,8},{16,20},{20,16},{24,28},{28,24},{32,36},... | collective-permute-start | bytes 1179656 | tf_op jit(solution)/shard_map/ppermute | solution.py:308
  126.2 15.6 %collective-permute-start.17 = (bf16[192,768]{1,0:T(8,128)(2,1)S(1)}, bf16[192,768]{1,0:T(8,128)(2,1)S(1)}, u32[]{:S(2)}, u32[]{:S(2)}) collective-permute-start(bf16[192,768]{1,0:T(8,128)(2,1)S(1)} %get-tuple-element.89.refs_4_), channel_id=1, source_target_pairs={{0,1},{1,2},{2,3},{3,0},{4,5},{5,6},{6,7},{7,4},{8,9},{9,10},{10,1... | collective-permute-start | bytes 884744 | tf_op jit(solution)/shard_map/ppermute | solution.py:272
  129.4 20.3 %collective-permute-start.22 = (bf16[192,768]{1,0:T(8,128)(2,1)S(1)}, bf16[192,768]{1,0:T(8,128)(2,1)S(1)}, u32[]{:S(2)}, u32[]{:S(2)}) collective-permute-start(bf16[192,768]{1,0:T(8,128)(2,1)S(1)} %get-tuple-element.90.refs_8_), channel_id=1, source_target_pairs={{0,3},{1,0},{2,1},{3,2},{4,7},{5,4},{6,5},{7,6},{8,11},{9,8},{10,9... | collective-permute-start | bytes 884744 | tf_op jit(solution)/shard_map/ppermute | solution.py:272
  137.2 17.9 %collective-permute-start.21 = (bf16[192,768]{1,0:T(8,128)(2,1)S(1)}, bf16[192,768]{1,0:T(8,128)(2,1)S(1)}, u32[]{:S(2)}, u32[]{:S(2)}) collective-permute-start(bf16[192,768]{1,0:T(8,128)(2,1)S(1)} %get-tuple-element.90.refs_8_), channel_id=1, source_target_pairs={{0,2},{1,3},{2,0},{3,1},{4,6},{5,7},{6,4},{7,5},{8,10},{9,11},{10,... | collective-permute-start | bytes 884744 | tf_op jit(solution)/shard_map/ppermute | solution.py:272
  137.2 18.0 %collective-permute-start.20 = (bf16[192,768]{1,0:T(8,128)(2,1)S(1)}, bf16[192,768]{1,0:T(8,128)(2,1)S(1)}, u32[]{:S(2)}, u32[]{:S(2)}) collective-permute-start(bf16[192,768]{1,0:T(8,128)(2,1)S(1)} %get-tuple-element.90.refs_8_), channel_id=1, source_target_pairs={{0,1},{1,2},{2,3},{3,0},{4,5},{5,6},{6,7},{7,4},{8,9},{9,10},{10,1... | collective-permute-start | bytes 884744 | tf_op jit(solution)/shard_map/ppermute | solution.py:272
  141.8 15.3 %collective-permute-start.25 = (bf16[192,512]{1,0:T(8,128)(2,1)S(1)}, bf16[192,512]{1,0:T(8,128)(2,1)S(1)}, u32[]{:S(2)}, u32[]{:S(2)}) collective-permute-start(bf16[192,512]{1,0:T(8,128)(2,1)S(1)} %get-tuple-element.91.refs_12_), channel_id=1, source_target_pairs={{0,3},{1,0},{2,1},{3,2},{4,7},{5,4},{6,5},{7,6},{8,11},{9,8},{10,9... | collective-permute-start | bytes 589832 | tf_op jit(solution)/shard_map/ppermute | solution.py:272
  149.7 13.9 %collective-permute-start.23 = (bf16[192,512]{1,0:T(8,128)(2,1)S(1)}, bf16[192,512]{1,0:T(8,128)(2,1)S(1)}, u32[]{:S(2)}, u32[]{:S(2)}) collective-permute-start(bf16[192,512]{1,0:T(8,128)(2,1)S(1)} %get-tuple-element.91.refs_12_), channel_id=1, source_target_pairs={{0,1},{1,2},{2,3},{3,0},{4,5},{5,6},{6,7},{7,4},{8,9},{9,10},{10,1... | collective-permute-start | bytes 589832 | tf_op jit(solution)/shard_map/ppermute | solution.py:272
  157.1 9.8 %collective-permute-start.26 = (bf16[192,256]{1,0:T(8,128)(2,1)S(1)}, bf16[192,256]{1,0:T(8,128)(2,1)S(1)}, u32[]{:S(2)}, u32[]{:S(2)}) collective-permute-start(bf16[192,256]{1,0:T(8,128)(2,1)S(1)} %get-tuple-element.92.refs_16_), channel_id=1, source_target_pairs={{0,1},{1,2},{2,3},{3,0},{4,5},{5,6},{6,7},{7,4},{8,9},{9,10},{10,1... | collective-permute-start | bytes 294920 | tf_op jit(solution)/shard_map/ppermute | solution.py:272
  (13 other events, 125.3 us)
